TPU v7x, 32 devices: a whole 2x2x4 slice. The times are simulated.
32 devices in a mesh: blk: 8 (over z, y), dp: 4 (over x, core).
Axes of the slice: x: 2, y: 2, z: 4, core: 2. Of those that a mesh axis runs over, the one named last changes fastest.
Arguments:
- memory: float32 [65536, 172], P(('blk', 'dp')), may hold values from -3 to 3
- src: int32 [2, 4096], P(None, ('blk', 'dp')), may hold values from 0 to 2047, as said below
- dst: int32 [2, 4096], P(None, ('blk', 'dp')), may hold values from 0 to 2047, as said below
- negative: int32 [2, 4096], P(None, ('blk', 'dp')), may hold values from 0 to 2047
- event_time: int32 [2, 4096], P(None, ('blk', 'dp')), may hold values from 0 to 1023
- neighbours: int32 [2, 10, 12288], P(None, None, ('blk', 'dp')), may hold values from 0 to 2047
- neighbour_time: int32 [2, 10, 12288], P(None, None, ('blk', 'dp')), may hold values from 0 to 1023
- time_omega: float32 [100], replicated, may hold values from 0.001 to 1
- w_input: float32 [444, 516], replicated, may hold values from -0.25 to 0.25
- w_hidden: float32 [172, 516], replicated, may hold values from -0.4375 to 0.4375
- gru_bias: float32 [2, 516], replicated, may hold values from -3 to 3
- w_query: float32 [172, 172], replicated, may hold values from -0.4807515 to 0.4807515
- w_keyval: float32 [272, 344], replicated, may hold values from -0.7508627 to 0.7508627
- w_decode: float32 [172], replicated, may hold values from -0.875 to 0.875
Outputs:
- memory_out: float32 [65536, 172], P(('blk', 'dp'))
- losses: float32 [2], replicated
- w_input_out: float32 [444, 516], replicated
- w_hidden_out: float32 [172, 516], replicated
- gru_bias_out: float32 [2, 516], replicated
- w_query_out: float32 [172, 172], replicated
- w_keyval_out: float32 [272, 344], replicated
- w_decode_out: float32 [172], replicated
Inputs may be any that keep to these rules, and one draw needn't show every extreme that they name: In each step and event block, the 128 src and 128 dst entries are 256 different rows. `dst`: different from every src entry of the same step and event block, and from each other.
All inputs are finite; a program needn't handle non-finite values.
Results may differ from a plain program's by a relative error of at most 0.00012.
Values sent between devices are 32-bit elements; how exact they have to be, the bound alone decides.
No kernel may reach another device: no remote copies, remote signals or barrier semaphores. Data moves between devices by JAX's collectives and lax.ppermute only.
A program may use at most 128 MiB of HBM per device.

v0:
```python
import jax
import jax.numpy as jnp
from jax import lax
from jax.sharding import PartitionSpec as P

HEADS = 2
STEPS = 2
rate = 0.25
exact = lax.Precision.HIGHEST


def passed_along(shard, axis, by):
    devices = lax.axis_size(axis)
    return lax.ppermute(shard, axis, [(i, (i + by) % devices) for i in range(devices)])


def step_loss(params, memory, src_ids, dst_ids, neg_ids, times, nbr_ids, nbr_times, omega, count):
    w_input, w_hidden, gru_bias, w_query, w_keyval, w_decode = params
    width = memory.shape[1]
    events = src_ids.shape[0]
    h_src = memory[src_ids]
    h_dst = memory[dst_ids]
    stamp = times.astype(jnp.float32)
    tenc = jnp.cos(stamp[:, None] * omega[None, :])
    inputs = jnp.concatenate(
        [jnp.concatenate([h_src, h_dst, tenc], 1), jnp.concatenate([h_dst, h_src, tenc], 1)], 0
    )
    hidden = jnp.concatenate([h_src, h_dst], 0)
    gate_in = (
        jnp.dot(inputs, w_input, precision=exact, preferred_element_type=jnp.float32) + gru_bias[0]
    )
    gate_hid = (
        jnp.dot(hidden, w_hidden, precision=exact, preferred_element_type=jnp.float32) + gru_bias[1]
    )
    reset = jax.nn.sigmoid(gate_in[:, :width] + gate_hid[:, :width])
    update = jax.nn.sigmoid(gate_in[:, width : 2 * width] + gate_hid[:, width : 2 * width])
    cand = jnp.tanh(gate_in[:, 2 * width :] + reset * gate_hid[:, 2 * width :])
    fresh = (1.0 - update) * cand + update * hidden
    touched = jnp.concatenate([src_ids, dst_ids], 0)
    updated = memory.at[touched].set(fresh)
    query_ids = jnp.concatenate([src_ids, dst_ids, neg_ids], 0)
    query_mem = updated[query_ids]
    rows = query_ids.shape[0]
    row_time = jnp.concatenate([stamp, stamp, stamp], 0)
    nbr_mem = updated[nbr_ids]
    delta = row_time[None, :] - nbr_times.astype(jnp.float32)
    nenc = jnp.cos(delta[:, :, None] * omega[None, None, :])
    key_in = jnp.concatenate([nbr_mem, nenc], 2)
    count_nbr = key_in.shape[0]
    keyval = jnp.dot(
        key_in.reshape(count_nbr * rows, -1),
        w_keyval,
        precision=exact,
        preferred_element_type=jnp.float32,
    )
    keyval = keyval.reshape(count_nbr, rows, 2 * width)
    query = jnp.dot(query_mem, w_query, precision=exact, preferred_element_type=jnp.float32)
    head_size = width // HEADS
    keys = keyval[:, :, :width].reshape(count_nbr, rows, HEADS, head_size)
    values = keyval[:, :, width:].reshape(count_nbr, rows, HEADS, head_size)
    query = query.reshape(rows, HEADS, head_size)
    scores = jnp.sum(keys * query[None], -1) / jnp.sqrt(jnp.float32(head_size))
    top = jnp.max(scores, 0, keepdims=True)
    probs = jnp.exp(scores - top)
    probs = probs / jnp.sum(probs, 0, keepdims=True)
    attn = jnp.sum(probs[:, :, :, None] * values, 0).reshape(rows, width)
    embed = query_mem + attn
    e_src = embed[:events]
    e_dst = embed[events : 2 * events]
    e_neg = embed[2 * events :]
    pos = jnp.sum(e_src * e_dst * w_decode[None, :], 1)
    neg = jnp.sum(e_src * e_neg * w_decode[None, :], 1)
    loss = jnp.sum(jax.nn.softplus(-pos) + jax.nn.softplus(neg)) / count
    return (loss, (updated, fresh))


def summed_terms(grads, loss):
    result = lax.psum(tuple(grads) + (loss,), ("blk", "dp"))
    return (tuple(result[:-1]), result[-1])


def on_device(
    memory,
    src,
    dst,
    negative,
    event_time,
    neighbours,
    neighbour_time,
    time_omega,
    w_input,
    w_hidden,
    gru_bias,
    w_query,
    w_keyval,
    w_decode,
):
    params = (w_input, w_hidden, gru_bias, w_query, w_keyval, w_decode)
    count = jnp.float32(src.shape[1] * lax.axis_size("blk") * lax.axis_size("dp"))
    losses = []
    for step in range(STEPS):
        current = memory
        fn = lambda p: step_loss(
            p,
            current,
            src[step],
            dst[step],
            negative[step],
            event_time[step],
            neighbours[step],
            neighbour_time[step],
            time_omega,
            count,
        )
        loss, back, extra = jax.vjp(fn, params, has_aux=True)
        updated, fresh = extra
        grads = back(jnp.float32(1.0))[0]
        sums, total = summed_terms(grads, loss)
        params = tuple((p - rate * g for p, g in zip(params, sums)))
        losses.append(total)
        memory = passed_along(updated, "blk", 1)
    return (
        memory,
        jnp.stack(losses),
        params[0],
        params[1],
        params[2],
        params[3],
        params[4],
        params[5],
    )


def solution(mesh):
    return jax.shard_map(
        on_device,
        mesh=mesh,
        in_specs=(
            P(("blk", "dp"), None),
            P(None, ("blk", "dp")),
            P(None, ("blk", "dp")),
            P(None, ("blk", "dp")),
            P(None, ("blk", "dp")),
            P(None, None, ("blk", "dp")),
            P(None, None, ("blk", "dp")),
            P(),
            P(),
            P(),
            P(),
            P(),
            P(),
            P(),
        ),
        out_specs=(P(("blk", "dp"), None), P(), P(), P(), P(), P(), P(), P()),
        check_vma=False,
    )
```

profile of v0, /device:TPU:0, one launch (start us, length us, event | category | flops | bytes accessed | tf_op | source)
XLA Modules:
  0.0 648.8 jit_solution(14372013255026179732)
XLA Ops:
  21.8 3.3 gather_fusion
  38.6 3.2 collective-permute-start
  47.1 10.0 %gather_fusion.6 = f32[3840,172]{1,0:T(8,128)} fusion(f32[2048,172]{1,0:T(8,128)S(1)} %scatter_fusion, s32[4096]{0:T(1024)S(1)} %pad_clamp_fusion.1), kind=kCustom, calls=%fused_computation.6 | custom fusion | bytes 5299200 | tf_op jit(solution)/shard_map/jvp()/gather | solution.py:45
  57.2 3.5 copy.82
  60.7 12.4 %multiply_cosine_fusion = (f32[10,384,100]{1,2,0:T(8,128)}, f32[10,384,100]{1,2,0:T(8,128)S(1)}) fusion(f32[10,384]{1,0:T(8,128)S(1)} %fusion.64, f32[100]{0:T(128)} %param.22, f32[10,384]{1,0:T(8,128)S(1)} %fusion.66), kind=kLoop, calls=%fused_computation.40 | loop fusion | flops 768000 | bytes 3103120 | tf_op jit(solution)/shard_map/jvp()/cos | solution.py:47
  73.1 9.6 %fusion.5 = f32[10,384,344]{1,2,0:T(8,128)S(1)} fusion(f32[10,384,100]{1,2,0:T(8,128)S(1)} %get-tuple-element.135, f32[10,384,172]{1,2,0:T(8,128)S(1)} %copy.82, f32[272,344]{1,0:T(8,128)S(1)} %copy-done.18), kind=kOutput, calls=%fused_computation.29 | convolution fusion | flops 4312657920 | bytes 9836032 | tf_op jit(solution)/shard_map/jvp()/dot_general | solution.py:50
  95.7 3.8 multiply_reduce_fusion.6
  112.4 4.6 multiply_reduce_fusion.4
  119.9 10.7 %fusion.7 = f32[272,344]{1,0:T(8,128)} fusion(f32[10,384,172]{1,2,0:T(8,128)} %get-tuple-element.101, f32[10,384,172]{1,2,0:T(8,128)} %broadcast_multiply_fusion.3, f32[10,384,100]{1,2,0:T(8,128)} %copy-done.14, f32[10,384,172]{1,2,0:T(8,128)S(1)} %copy-done.6), kind=kOutput, calls=%fused_computation.51 | convolution fusion | flops 4313978880 | bytes 9836032 | tf_op jit(solution)/shard_map/transpose(jvp())/dot_general | solution.py:50
  130.6 11.5 %fusion.1 = f32[10,384,172]{2,1,0:T(8,128)} fusion(f32[10,384,172]{1,2,0:T(8,128)S(1)} %copy-done.10, f32[10,384,172]{1,2,0:T(8,128)S(1)} %copy-done.8, f32[272,344,1]{1,0,2:T(8,128)S(1)} %bitcast.110), kind=kOutput, calls=%fused_computation.23 | convolution fusion | flops 2727782400 | bytes 8318976 | tf_op jit(solution)/shard_map/transpose(jvp())/split | solution.py:48
  142.2 21.5 %scatter_custom_fusion.3 = f32[2048,172]{1,0:T(8,128)S(1)} fusion(s32[3840]{0:T(1024)} %copy-done.82, f32[3840,172]{1,0:T(8,128)} %bitcast.112, f32[]{:T(128)} %constant.19.clone.1), kind=kCustom, calls=%fused_computation.62 | custom fusion | flops 660480 | bytes 1409536 | tf_op jit(solution)/shard_map/transpose(jvp())/scatter-add | solution.py:45
  163.7 4.5 scatter_custom_fusion.4
  168.2 3.2 add_any.97
  183.0 41.2 %all-reduce.23 = (f32[2,516]{1,0:T(2,128)S(1)}, f32[172]{0:T(256)S(1)}) all-reduce(f32[2,516]{1,0:T(2,128)S(1)} %pad_add_fusion.25, f32[172]{0:T(256)S(1)} %add_any.104), channel_id=1, replica_groups=mesh['blk'=8,'dp'=4] {'blk','dp'}, use_global_device_ids=true, to_apply=%region_19.21 | all-reduce | flops 1204 | bytes 9632 | tf_op jit(solution)/shard_map/psum | solution.py:78
  227.8 87.3 %all-reduce.31.cloned.1.call-done = (f32[444,516]{0,1:T(8,128)}, f32[172,516]{1,0:T(8,128)}, f32[272,344]{1,0:T(8,128)}, f32[172,172]{1,0:T(8,128)}) async-done(((f32[444,516]{0,1:T(8,128)}, f32[172,516]{1,0:T(8,128)}, f32[272,344]{1,0:T(8,128)}, f32[172,172]{1,0:T(8,128)}), (f32[444,516]{0,1:T(8,128)}, f32[172,516]{1,0:T(8,128)}, f32[272,344]{1,0:T(8,128)}, ...) | async-done | bytes 1764048 | tf_op jit(solution)/shard_map/psum | solution.py:78
  345.5 10.5 %gather_fusion.10 = f32[3840,172]{1,0:T(8,128)} fusion(f32[2048,172]{1,0:T(8,128)S(1)} %scatter_fusion.1, s32[4096]{0:T(1024)} %pad_clamp_fusion), kind=kCustom, calls=%fused_computation.10 | custom fusion | bytes 5299200 | tf_op jit(solution)/shard_map/jvp()/gather | solution.py:45
  356.1 5.1 copy.94
  361.2 10.7 %fusion.4 = f32[10,384,344]{1,2,0:T(8,128)S(1)} fusion(f32[272,344,1]{1,0,2:T(8,128)} %fusion.58, f32[10,384,100]{1,2,0:T(8,128)} %get-tuple-element.134, f32[10,384,172]{1,2,0:T(8,128)} %copy.94), kind=kOutput, calls=%fused_computation.28 | convolution fusion | flops 4312657920 | bytes 9836032 | tf_op jit(solution)/shard_map/jvp()/dot_general | solution.py:50
  376.0 3.7 reshape.874
  384.3 3.7 mul.489
  388.0 4.7 fusion.115
  399.2 3.7 reshape.876
  406.9 3.9 broadcast_in_dim.101
  416.0 7.8 %fusion.6 = f32[272,344]{1,0:T(8,128)} fusion(f32[10,384,172]{1,2,0:T(8,128)S(1)} %get-tuple-element.99, f32[10,384,172]{1,2,0:T(8,128)S(1)} %copy-done.9, f32[10,384,100]{1,2,0:T(8,128)S(1)} %copy-done.13, f32[10,384,172]{1,2,0:T(8,128)S(1)} %copy-done.7), kind=kOutput, calls=%fused_computation.50 | convolution fusion | flops 4313978880 | bytes 9836032 | tf_op jit(solution)/shard_map/transpose(jvp())/dot_general | solution.py:50
  423.8 11.8 %fusion.3 = f32[10,384,172]{2,1,0:T(8,128)} fusion(f32[10,384,172]{1,2,0:T(8,128)S(1)} %get-tuple-element.99, f32[10,384,172]{1,2,0:T(8,128)S(1)} %copy-done.9, f32[272,344,1]{1,0,2:T(8,128)S(1)} %copy-done.29), kind=kOutput, calls=%fused_computation.25 | convolution fusion | flops 2727782400 | bytes 8318976 | tf_op jit(solution)/shard_map/transpose(jvp())/split | solution.py:48
  436.5 22.2 %scatter_custom_fusion.6 = f32[2048,172]{1,0:T(8,128)} fusion(s32[3840]{0:T(1024)} %copy-done.81, f32[3840,172]{1,0:T(8,128)} %bitcast.111, f32[]{:T(128)} %constant.19.clone.1), kind=kCustom, calls=%fused_computation.58 | custom fusion | flops 660480 | bytes 1409536 | tf_op jit(solution)/shard_map/transpose(jvp())/scatter-add | solution.py:45
  458.8 4.7 scatter_custom_fusion.7
  463.5 3.8 add_any.112
  467.3 3.4 gather_fusion.11
  475.4 3.3 fusion.25
  486.0 67.1 %all-reduce.22 = (f32[1]{0:T(128)}, f32[1]{0:T(128)}, f32[2,516]{1,0:T(2,128)S(1)}, f32[172]{0:T(256)S(1)}) all-reduce(f32[1]{0:T(128)} %bitcast.27, f32[1]{0:T(128)} %bitcast.20, f32[2,516]{1,0:T(2,128)S(1)} %pad_add_fusion.24, f32[172]{0:T(256)S(1)} %add_any.119), channel_id=1, replica_groups=mesh['blk'=8,'dp'=4] {'blk','dp'}, use_global_device_ids=true, to_apply=%region_36.38 | all-reduce | flops 1206 | bytes 9648 | tf_op jit(solution)/shard_map/psum | solution.py:78
  556.1 75.7 %all-reduce.29.cloned.1.call-done = (f32[444,516]{0,1:T(8,128)}, f32[172,516]{1,0:T(8,128)}, f32[172,172]{1,0:T(8,128)}, f32[272,344]{1,0:T(8,128)}) async-done(((f32[444,516]{0,1:T(8,128)}, f32[172,516]{1,0:T(8,128)}, f32[172,172]{1,0:T(8,128)}, f32[272,344]{1,0:T(8,128)}), (f32[444,516]{0,1:T(8,128)}, f32[172,516]{1,0:T(8,128)}, f32[172,172]{1,0:T(8,128)}, ...) | async-done | bytes 1764048 | tf_op jit(solution)/shard_map/psum | solution.py:78
  (398 shorter events, 155.0 us)
Async XLA Ops:
  7.2 308.0 %all-reduce.31.cloned.1.call-start = ((), (), s32[]{:S(2)}) async-start(), calls=%async_computation.1 | async-start | bytes 4227072 | tf_op jit(solution)/shard_map/psum | solution.py:78
  7.2 25.1 %copy-start.90 = (u32[256]{0:T(256)}, u32[256]{0:T(256)S(1)}, u32[]{:S(2)}) copy-start(u32[256]{0:T(256)S(1)} %iota_add_fusion) | copy-start | bytes 3076
  12.0 9.8 %copy-start.99 = (s32[1024]{0:T(1024)}, s32[1024]{0:T(1024)S(1)}, u32[]{:S(2)}) copy-start(s32[1024]{0:T(1024)S(1)} %pad_clamp_fusion.9) | copy-start | bytes 12292
  15.4 12.5 %copy-start.50 = (f32[128,172]{1,0:T(8,128)}, f32[128,172]{1,0:T(8,128)S(1)}, u32[]{:S(2)}) copy-start(f32[128,172]{1,0:T(8,128)S(1)} %gather_fusion.2) | copy-start | bytes 264196
  15.5 16.8 %copy-start.33 = (f32[128,172]{0,1:T(8,128)}, f32[128,172]{0,1:T(8,128)S(1)}, u32[]{:S(2)}) copy-start(f32[128,172]{0,1:T(8,128)S(1)} %copy.73) | copy-start | bytes 264196
  16.4 16.0 %copy-start.35 = (f32[128,172]{0,1:T(8,128)}, f32[128,172]{0,1:T(8,128)S(1)}, u32[]{:S(2)}) copy-start(f32[128,172]{0,1:T(8,128)S(1)} %copy.72) | copy-start | bytes 264196
  38.6 278.4 %collective-permute-start = (f32[2048,172]{0,1:T(8,128)}, f32[2048,172]{0,1:T(8,128)}, u32[]{:S(2)}, u32[]{:S(2)}) collective-permute-start(f32[2048,172]{0,1:T(8,128)} %copy.75), channel_id=1, source_target_pairs={{0,4},{4,8},{8,12},{12,16},{16,20},{20,24},{24,28},{28,0},{1,5},{5... | collective-permute-start | bytes 4227080 | tf_op jit(solution)/shard_map/ppermute | solution.py:14
  46.3 10.9 %copy-start.30 = (f32[384,172]{0,1:T(8,128)}, f32[384,172]{0,1:T(8,128)S(1)}, u32[]{:S(2)}) copy-start(f32[384,172]{0,1:T(8,128)S(1)} %fusion.117) | copy-start | bytes 792580
  60.6 22.1 %copy-start.5 = (f32[10,384,172]{1,2,0:T(8,128)}, f32[10,384,172]{1,2,0:T(8,128)S(1)}, u32[]{:S(2)}) copy-start(f32[10,384,172]{1,2,0:T(8,128)S(1)} %copy.82) | copy-start | bytes 7925764
  60.7 12.5 %copy-start.18 = (f32[272,344]{1,0:T(8,128)S(1)}, f32[272,344]{1,0:T(8,128)}, u32[]{:S(2)}) copy-start(f32[272,344]{1,0:T(8,128)} %param.27) | copy-start | bytes 1122820
  73.1 9.6 %copy-start.14 = (f32[10,384,100]{1,2,0:T(8,128)}, f32[10,384,100]{1,2,0:T(8,128)S(1)}, u32[]{:S(2)}) copy-start(f32[10,384,100]{1,2,0:T(8,128)S(1)} %get-tuple-element.135) | copy-start | bytes 4608004
  119.9 10.7 %copy-start.8 = (f32[10,384,172]{1,2,0:T(8,128)S(1)}, f32[10,384,172]{1,2,0:T(8,128)}, u32[]{:S(2)}) copy-start(f32[10,384,172]{1,2,0:T(8,128)} %broadcast_multiply_fusion.3) | copy-start | bytes 7925764
  119.9 10.7 %copy-start.10 = (f32[10,384,172]{1,2,0:T(8,128)S(1)}, f32[10,384,172]{1,2,0:T(8,128)}, u32[]{:S(2)}) copy-start(f32[10,384,172]{1,2,0:T(8,128)} %get-tuple-element.101) | copy-start | bytes 7925764
  178.6 45.5 %copy-start.109 = (s32[128]{0:T(128)S(1)}, s32[128]{0:T(128)}, u32[]{:S(2)}) copy-start(s32[128]{0:T(128)} %get-tuple-element.130) | copy-start | bytes 1540
  178.7 46.1 %copy-start.108 = (s32[128]{0:T(128)S(1)}, s32[128]{0:T(128)}, u32[]{:S(2)}) copy-start(s32[128]{0:T(128)} %get-tuple-element.128) | copy-start | bytes 1540
  178.7 46.7 %copy-start.113 = (s32[128]{0:T(128)S(1)}, s32[128]{0:T(128)}, u32[]{:S(2)}) copy-start(s32[128]{0:T(128)} %get-tuple-element.120) | copy-start | bytes 1540
  178.7 46.7 %copy-start.114 = (s32[128]{0:T(128)S(1)}, s32[128]{0:T(128)}, u32[]{:S(2)}) copy-start(s32[128]{0:T(128)} %get-tuple-element.142) | copy-start | bytes 1540
  178.7 453.1 %all-reduce.29.cloned.1.call-start = ((), (), s32[]{:S(2)}) async-start(), calls=%async_computation | async-start | bytes 4227072 | tf_op jit(solution)/shard_map/psum | solution.py:78
  179.0 48.2 %copy-start.89 = (f32[2,516]{1,0:T(2,128)S(1)}, f32[2,516]{1,0:T(2,128)}, u32[]{:S(2)}) copy-start(f32[2,516]{1,0:T(2,128)} %param.25) | copy-start | bytes 12388
  179.0 48.2 %copy-start.97 = (f32[172]{0:T(256)S(1)}, f32[172]{0:T(256)}, u32[]{:S(2)}) copy-start(f32[172]{0:T(256)} %param.28) | copy-start | bytes 2068
  179.1 137.8 %copy-start.98 = (s32[1024]{0:T(1024)}, s32[1024]{0:T(1024)S(1)}, u32[]{:S(2)}) copy-start(s32[1024]{0:T(1024)S(1)} %pad_clamp_fusion.6) | copy-start | bytes 12292
  181.2 135.8 %copy-start.3 = (u32[2048,172]{1,0:T(8,128)}, u32[2048,172]{1,0:T(8,128)S(1)}, u32[]{:S(2)}) copy-start(u32[2048,172]{1,0:T(8,128)S(1)} %scatter_custom_fusion) | copy-start | bytes 4227076
  181.2 138.6 %copy-start.81 = (s32[3840]{0:T(1024)}, s32[3840]{0:T(1024)S(1)}, u32[]{:S(2)}) copy-start(s32[3840]{0:T(1024)S(1)} %reshape.961) | copy-start | bytes 46084
  183.0 136.8 %copy-start.100 = (s32[384]{0:T(512)}, s32[384]{0:T(512)S(1)}, u32[]{:S(2)}) copy-start(s32[384]{0:T(512)S(1)} %fusion.70) | copy-start | bytes 4612
  227.2 92.6 %copy-start.85 = (f32[2,516]{1,0:T(2,128)}, f32[2,516]{1,0:T(2,128)S(1)}, u32[]{:S(2)}) copy-start(f32[2,516]{1,0:T(2,128)S(1)} %multiply_subtract_fusion.11) | copy-start | bytes 12388
  480.2 72.9 %copy-start.93 = (f32[172]{0:T(256)S(1)}, f32[172]{0:T(256)}, u32[]{:S(2)}) copy-start(f32[172]{0:T(256)} %multiply_subtract_fusion.13) | copy-start | bytes 2068
  480.2 75.3 %copy-start.86 = (f32[2,516]{1,0:T(2,128)S(1)}, f32[2,516]{1,0:T(2,128)}, u32[]{:S(2)}) copy-start(f32[2,516]{1,0:T(2,128)} %copy-done.85) | copy-start | bytes 12388
  480.3 151.6 %copy-start.25 = (f32[172,172]{1,0:T(8,128)S(1)}, f32[172,172]{1,0:T(8,128)}, u32[]{:S(2)}) copy-start(f32[172,172]{1,0:T(8,128)} %param.26) | copy-start | bytes 355012
  482.5 153.2 %copy-start.28 = (f32[172,516]{1,0:T(8,128)S(1)}, f32[172,516]{1,0:T(8,128)}, u32[]{:S(2)}) copy-start(f32[172,516]{1,0:T(8,128)} %param.24) | copy-start | bytes 1065028
  482.5 153.2 %copy-start.42 = (f32[172,516]{1,0:T(8,128)S(1)}, f32[172,516]{1,0:T(8,128)}, u32[]{:S(2)}) copy-start(f32[172,516]{1,0:T(8,128)} %get-tuple-element.73) | copy-start | bytes 1065028
  482.5 155.0 %copy-start.26 = (f32[444,516]{0,1:T(8,128)S(1)}, f32[444,516]{0,1:T(8,128)}, u32[]{:S(2)}) copy-start(f32[444,516]{0,1:T(8,128)} %get-tuple-element.72) | copy-start | bytes 2749252
  482.5 156.4 %collective-permute-start.1 = (f32[2048,172]{0,1:T(8,128)}, f32[2048,172]{0,1:T(8,128)}, u32[]{:S(2)}, u32[]{:S(2)}) collective-permute-start(f32[2048,172]{0,1:T(8,128)} %copy.91), channel_id=1, source_target_pairs={{0,4},{4,8},{8,12},{12,16},{16,20},{20,24},{24,28},{28,0},{1,5},{5... | collective-permute-start | bytes 4227080 | tf_op jit(solution)/shard_map/ppermute | solution.py:14
  (90 other events, 345.7 us)
Sparse Core Ops, SparseCore 0:
  178.7 136.3 all-reduce.30
  480.4 151.4 all-reduce.28
where the time goes:
time: 657 us; the launch traced here: 649 us
  waiting for transfers between devices  163 us (25%)
  other arithmetic  141 us (21%)
  local copies, waits for them, and re-layouts  129 us (20%)
  blocking collectives  108 us (16%)
  matrix products  85.7 us (13%)
  between operations  17.4 us (3%)
    psum x2, waiting for transfers between devices, summed_terms(): result = lax.psum(tuple(grads) + (loss,), ('blk', 'dp'))  163 us
    psum x2, blocking collectives, summed_terms(): result = lax.psum(tuple(grads) + (loss,), ('blk', 'dp'))  108 us
    scatter-add x2, other arithmetic, step_loss(): nbr_mem = updated[nbr_ids]  43.8 us
    dot_general x4, matrix products, step_loss(): jnp.dot(key_in.reshape(count_nbr * rows, -1), w_keyval, precision=exact,...  38.8 us
    gather x4, local copies, waits for them, and re-layouts, step_loss(): nbr_mem = updated[nbr_ids]  29.1 us
    split x2, matrix products, step_loss(): key_in = jnp.concatenate([nbr_mem, nenc], 2)  23.3 us
    gather x8, local copies, waits for them, and re-layouts, step_loss(): updated = memory.at[touched].set(fresh)  14.9 us
    unnamed x238, local copies, waits for them, and re-layouts  13.9 us
  transfers between devices with their start and end apart: 4, of which 2 were waited for; matrix products, arithmetic and copies ran while one was open for 24% of the time, Pallas kernels for 0%

commit v1 on v0

--- a/solution.py
+++ b/solution.py
@@ -75,7 +75,7 @@
 
 
 def summed_terms(grads, loss):
-    result = lax.psum(tuple(grads) + (loss,), ("blk", "dp"))
+    result = lax.psum(lax.psum(tuple(grads) + (loss,), "dp"), "blk")
     return (tuple(result[:-1]), result[-1])
 
 

time: 657 us -> 724 us (1.10)
  waiting for transfers between devices: 163 us -> 215 us
  local copies, waits for them, and re-layouts: 129 us -> 144 us
  blocking collectives: 108 us -> 94.1 us
  other arithmetic: 141 us -> 152 us
    psum x2 -> x4, waiting for transfers between devices: 163 us -> 215 us  [summed_terms(): result = lax.psum(lax.psum(tuple(grads) + (loss,), 'dp'), 'blk')]
    psum x2 -> x4, blocking collectives: 108 us -> 94.1 us  [summed_terms(): result = lax.psum(lax.psum(tuple(grads) + (loss,), 'dp'), 'blk')]
    unnamed x238 -> x244, local copies, waits for them, and re-layouts: 13.9 us -> 15 us
  transfers between devices with their start and end apart: 4 -> 6, of which waited for: 2 -> 4; matrix products, arithmetic and copies ran while one was open for 24% -> 4% of each run, Pallas kernels for 0% -> 0%
where the time goes in v1:
time: 724 us; the launch traced here: 715 us
  waiting for transfers between devices  215 us (30%)
  other arithmetic  152 us (21%)
  local copies, waits for them, and re-layouts  144 us (20%)
  blocking collectives  94.1 us (13%)
  matrix products  88.7 us (12%)
  between operations  17 us (2%)
    psum x4, waiting for transfers between devices, summed_terms(): result = lax.psum(lax.psum(tuple(grads) + (loss,), 'dp'), 'blk')  215 us
    psum x4, blocking collectives, summed_terms(): result = lax.psum(lax.psum(tuple(grads) + (loss,), 'dp'), 'blk')  94.1 us
    scatter-add x2, other arithmetic, step_loss(): nbr_mem = updated[nbr_ids]  44.7 us
    dot_general x4, matrix products, step_loss(): jnp.dot(key_in.reshape(count_nbr * rows, -1), w_keyval, precision=exact,...  39.2 us
    gather x4, local copies, waits for them, and re-layouts, step_loss(): nbr_mem = updated[nbr_ids]  31.4 us
    split x2, matrix products, step_loss(): key_in = jnp.concatenate([nbr_mem, nenc], 2)  23.3 us
    gather x8, local copies, waits for them, and re-layouts, step_loss(): updated = memory.at[touched].set(fresh)  17.2 us
    unnamed x244, local copies, waits for them, and re-layouts  15 us
  transfers between devices with their start and end apart: 6, of which 4 were waited for; matrix products, arithmetic and copies ran while one was open for 4% of the time, Pallas kernels for 0%

profile of v1, /device:TPU:0, one launch (start us, length us, event | category | flops | bytes accessed | tf_op | source)
XLA Modules:
  0.0 715.0 jit_solution(16985010035170524822)
XLA Ops:
  52.1 10.6 %gather_fusion.6 = f32[3840,172]{1,0:T(8,128)} fusion(f32[2048,172]{1,0:T(8,128)S(1)} %scatter_fusion, s32[4096]{0:T(1024)} %pad_clamp_fusion.1), kind=kCustom, calls=%fused_computation.6 | custom fusion | bytes 5299200 | tf_op jit(solution)/shard_map/jvp()/gather | solution.py:45
  62.6 5.1 copy.82
  69.4 12.1 %multiply_cosine_fusion = (f32[10,384,100]{1,2,0:T(8,128)}, f32[10,384,100]{1,2,0:T(8,128)S(1)}) fusion(f32[10,384]{1,0:T(8,128)S(1)} %fusion.64, f32[100]{0:T(128)} %param.22, f32[10,384]{1,0:T(8,128)S(1)} %fusion.66), kind=kLoop, calls=%fused_computation.40 | loop fusion | flops 768000 | bytes 3103120 | tf_op jit(solution)/shard_map/jvp()/cos | solution.py:47
  81.6 9.6 %fusion.5 = f32[10,384,344]{1,2,0:T(8,128)S(1)} fusion(f32[10,384,100]{1,2,0:T(8,128)S(1)} %get-tuple-element.149, f32[10,384,172]{1,2,0:T(8,128)S(1)} %copy-done.6, f32[272,344]{1,0:T(8,128)S(1)} %copy-done.16), kind=kOutput, calls=%fused_computation.29 | convolution fusion | flops 4312657920 | bytes 9836032 | tf_op jit(solution)/shard_map/jvp()/dot_general | solution.py:50
  95.3 3.8 reshape.869
  103.7 3.7 mul.438
  107.4 4.7 multiply_reduce_fusion.6
  118.7 4.2 reshape.871
  130.6 4.4 multiply_reduce_fusion.4
  137.9 11.1 %fusion.7 = f32[272,344]{1,0:T(8,128)} fusion(f32[10,384,172]{1,2,0:T(8,128)} %get-tuple-element.115, f32[10,384,172]{1,2,0:T(8,128)} %broadcast_multiply_fusion.3, f32[10,384,100]{1,2,0:T(8,128)} %copy-done.13, f32[10,384,172]{1,2,0:T(8,128)} %copy.82), kind=kOutput, calls=%fused_computation.51 | convolution fusion | flops 4313978880 | bytes 9836032 | tf_op jit(solution)/shard_map/transpose(jvp())/dot_general | solution.py:50
  149.1 11.5 %fusion.1 = f32[10,384,172]{2,1,0:T(8,128)} fusion(f32[10,384,172]{1,2,0:T(8,128)S(1)} %copy-done.10, f32[10,384,172]{1,2,0:T(8,128)S(1)} %copy-done.8, f32[272,344,1]{1,0,2:T(8,128)S(1)} %bitcast.110), kind=kOutput, calls=%fused_computation.23 | convolution fusion | flops 2727782400 | bytes 8318976 | tf_op jit(solution)/shard_map/transpose(jvp())/split | solution.py:48
  160.6 22.4 %scatter_custom_fusion.3 = f32[2048,172]{1,0:T(8,128)} fusion(s32[3840]{0:T(1024)} %copy-done.85, f32[3840,172]{1,0:T(8,128)} %bitcast.112, f32[]{:T(128)} %constant.19.clone.1), kind=kCustom, calls=%fused_computation.62 | custom fusion | flops 660480 | bytes 1409536 | tf_op jit(solution)/shard_map/transpose(jvp())/scatter-add | solution.py:45
  183.0 4.5 scatter_custom_fusion.4
  187.5 3.8 add_any.97
  211.0 48.0 %all-reduce.41.cloned.1.call-done = (f32[444,516]{0,1:T(8,128)}, f32[172,516]{1,0:T(8,128)}, f32[272,344]{1,0:T(8,128)}, f32[172,172]{1,0:T(8,128)}) async-done(((f32[444,516]{0,1:T(8,128)}, f32[172,516]{1,0:T(8,128)}, f32[272,344]{1,0:T(8,128)}, f32[172,172]{1,0:T(8,128)}), (f32[444,516]{0,1:T(8,128)}, f32[172,516]{1,0:T(8,128)}, f32[272,344]{1,0:T(8,128)}, ...) | async-done | bytes 1764048 | tf_op jit(solution)/shard_map/psum | solution.py:78
  263.2 5.9 all-reduce.27
  269.1 23.3 %all-reduce.23 = (f32[2,516]{1,0:T(2,128)S(1)}, f32[172]{0:T(256)S(1)}) all-reduce(f32[2,516]{1,0:T(2,128)S(1)} %get-tuple-element.80, f32[172]{0:T(256)S(1)} %get-tuple-element.81), channel_id=1, replica_groups=mesh['blk'=8,'dp'=4] {'blk'}, use_global_device_ids=true, to_apply=%region_21.23 | all-reduce | flops 1204 | bytes 9632 | tf_op jit(solution)/shard_map/psum | solution.py:78
  306.2 60.2 %all-reduce.37.cloned.1.call-done = (f32[444,516]{0,1:T(8,128)}, f32[172,516]{1,0:T(8,128)}, f32[272,344]{1,0:T(8,128)}, f32[172,172]{1,0:T(8,128)}) async-done(((f32[444,516]{0,1:T(8,128)}, f32[172,516]{1,0:T(8,128)}, f32[272,344]{1,0:T(8,128)}, f32[172,172]{1,0:T(8,128)}), (f32[444,516]{0,1:T(8,128)}, f32[172,516]{1,0:T(8,128)}, f32[272,344]{1,0:T(8,128)}, ...) | async-done | bytes 1764048 | tf_op jit(solution)/shard_map/psum | solution.py:78
  384.3 10.6 %gather_fusion.10 = f32[3840,172]{1,0:T(8,128)} fusion(f32[2048,172]{1,0:T(8,128)S(1)} %scatter_fusion.1, s32[4096]{0:T(1024)} %pad_clamp_fusion), kind=kCustom, calls=%fused_computation.10 | custom fusion | bytes 5299200 | tf_op jit(solution)/shard_map/jvp()/gather | solution.py:45
  394.9 5.1 copy.94
  400.0 10.7 %fusion.4 = f32[10,384,344]{1,2,0:T(8,128)S(1)} fusion(f32[272,344,1]{1,0,2:T(8,128)} %fusion.58, f32[10,384,100]{1,2,0:T(8,128)} %get-tuple-element.148, f32[10,384,172]{1,2,0:T(8,128)} %copy.94), kind=kOutput, calls=%fused_computation.28 | convolution fusion | flops 4312657920 | bytes 9836032 | tf_op jit(solution)/shard_map/jvp()/dot_general | solution.py:50
  426.8 4.7 fusion.115
  445.7 3.9 broadcast_in_dim.101
  454.8 7.8 %fusion.6 = f32[272,344]{1,0:T(8,128)} fusion(f32[10,384,172]{1,2,0:T(8,128)S(1)} %get-tuple-element.113, f32[10,384,172]{1,2,0:T(8,128)S(1)} %copy-done.9, f32[10,384,100]{1,2,0:T(8,128)S(1)} %copy-done.12, f32[10,384,172]{1,2,0:T(8,128)S(1)} %copy-done.7), kind=kOutput, calls=%fused_computation.50 | convolution fusion | flops 4313978880 | bytes 9836032 | tf_op jit(solution)/shard_map/transpose(jvp())/dot_general | solution.py:50
  462.6 11.7 %fusion.3 = f32[10,384,172]{2,1,0:T(8,128)} fusion(f32[10,384,172]{1,2,0:T(8,128)S(1)} %get-tuple-element.113, f32[10,384,172]{1,2,0:T(8,128)S(1)} %copy-done.9, f32[272,344,1]{1,0,2:T(8,128)S(1)} %copy-done.26), kind=kOutput, calls=%fused_computation.25 | convolution fusion | flops 2727782400 | bytes 8318976 | tf_op jit(solution)/shard_map/transpose(jvp())/split | solution.py:48
  475.3 22.2 %scatter_custom_fusion.6 = f32[2048,172]{1,0:T(8,128)} fusion(s32[3840]{0:T(1024)} %copy-done.84, f32[3840,172]{1,0:T(8,128)} %bitcast.111, f32[]{:T(128)} %constant.19.clone.1), kind=kCustom, calls=%fused_computation.58 | custom fusion | flops 660480 | bytes 1409536 | tf_op jit(solution)/shard_map/transpose(jvp())/scatter-add | solution.py:45
  497.5 4.7 scatter_custom_fusion.7
  502.2 3.8 add_any.112
  519.0 51.2 %all-reduce.39.cloned.1.call-done = (f32[444,516]{0,1:T(8,128)}, f32[172,516]{1,0:T(8,128)}, f32[172,172]{1,0:T(8,128)}, f32[272,344]{1,0:T(8,128)}) async-done(((f32[444,516]{0,1:T(8,128)}, f32[172,516]{1,0:T(8,128)}, f32[172,172]{1,0:T(8,128)}, f32[272,344]{1,0:T(8,128)}), (f32[444,516]{0,1:T(8,128)}, f32[172,516]{1,0:T(8,128)}, f32[172,172]{1,0:T(8,128)}, ...) | async-done | bytes 1764048 | tf_op jit(solution)/shard_map/psum | solution.py:78
  576.1 6.8 all-reduce.26
  582.8 58.2 %all-reduce.22 = (f32[1]{0:T(128)}, f32[1]{0:T(128)}, f32[2,516]{1,0:T(2,128)S(1)}, f32[172]{0:T(256)S(1)}) all-reduce(f32[1]{0:T(128)} %bitcast.27, f32[1]{0:T(128)} %bitcast.20, f32[2,516]{1,0:T(2,128)S(1)} %get-tuple-element.78, f32[172]{0:T(256)S(1)} %get-tuple-element.79), channel_id=1, replica_groups=mesh['blk'=8,'dp'=4] {'blk'}, use_global_device_ids=true, to_apply=%region_44.46 | all-reduce | flops 1206 | bytes 9648 | tf_op jit(solution)/shard_map/psum | solution.py:78
  644.1 55.1 %all-reduce.35.cloned.1.call-done = (f32[444,516]{0,1:T(8,128)}, f32[172,516]{1,0:T(8,128)}, f32[172,172]{1,0:T(8,128)}, f32[272,344]{1,0:T(8,128)}) async-done(((f32[444,516]{0,1:T(8,128)}, f32[172,516]{1,0:T(8,128)}, f32[172,172]{1,0:T(8,128)}, f32[272,344]{1,0:T(8,128)}), (f32[444,516]{0,1:T(8,128)}, f32[172,516]{1,0:T(8,128)}, f32[172,172]{1,0:T(8,128)}, ...) | async-done | bytes 1764048 | tf_op jit(solution)/shard_map/psum | solution.py:78
  (412 shorter events, 192.4 us)
Async XLA Ops:
  7.2 251.9 %all-reduce.41.cloned.1.call-start = ((), (), s32[]{:S(2)}) async-start(), calls=%async_computation.3 | async-start | bytes 4227072 | tf_op jit(solution)/shard_map/psum | solution.py:78
  7.2 32.5 %copy-start.93 = (u32[256]{0:T(256)}, u32[256]{0:T(256)S(1)}, u32[]{:S(2)}) copy-start(u32[256]{0:T(256)S(1)} %iota_add_fusion) | copy-start | bytes 3076
  13.9 16.2 %copy-start.102 = (s32[1024]{0:T(1024)}, s32[1024]{0:T(1024)S(1)}, u32[]{:S(2)}) copy-start(s32[1024]{0:T(1024)S(1)} %pad_clamp_fusion.9) | copy-start | bytes 12292
  21.1 14.1 %copy-start.77 = (f32[128,100]{1,0:T(8,128)}, f32[128,100]{1,0:T(8,128)S(1)}, u32[]{:S(2)}) copy-start(f32[128,100]{1,0:T(8,128)S(1)} %get-tuple-element.151) | copy-start | bytes 153604
  23.8 15.9 %copy-start.29 = (f32[128,172]{0,1:T(8,128)}, f32[128,172]{0,1:T(8,128)S(1)}, u32[]{:S(2)}) copy-start(f32[128,172]{0,1:T(8,128)S(1)} %copy.73) | copy-start | bytes 264196
  24.7 15.1 %copy-start.31 = (f32[128,172]{0,1:T(8,128)}, f32[128,172]{0,1:T(8,128)S(1)}, u32[]{:S(2)}) copy-start(f32[128,172]{0,1:T(8,128)S(1)} %copy.72) | copy-start | bytes 264196
  67.8 13.8 %copy-start.16 = (f32[272,344]{1,0:T(8,128)S(1)}, f32[272,344]{1,0:T(8,128)}, u32[]{:S(2)}) copy-start(f32[272,344]{1,0:T(8,128)} %param.27) | copy-start | bytes 1122820
  204.3 55.0 %copy-start.94 = (u32[256]{0:T(256)S(1)}, u32[256]{0:T(256)}, u32[]{:S(2)}) copy-start(u32[256]{0:T(256)} %copy-done.93) | copy-start | bytes 3076
  204.3 162.1 %all-reduce.37.cloned.1.call-start = ((), (), s32[]{:S(2)}) async-start(), calls=%async_computation.1 | async-start | bytes 4227072 | tf_op jit(solution)/shard_map/psum | solution.py:78
  206.0 55.3 %copy-start.83 = (s32[10,384]{1,0:T(8,128)S(1)}, s32[10,384]{1,0:T(8,128)}, u32[]{:S(2)}) copy-start(s32[10,384]{1,0:T(8,128)} %get-tuple-element.56) | copy-start | bytes 46084
  206.0 88.7 %collective-permute-start = (f32[2048,172]{0,1:T(8,128)}, f32[2048,172]{0,1:T(8,128)}, u32[]{:S(2)}, u32[]{:S(2)}) collective-permute-start(f32[2048,172]{0,1:T(8,128)} %copy.75), channel_id=1, source_target_pairs={{0,4},{4,8},{8,12},{12,16},{16,20},{20,24},{24,28},{28,0},{1,5},{5... | collective-permute-start | bytes 4227080 | tf_op jit(solution)/shard_map/ppermute | solution.py:14
  259.1 33.2 %copy-start.116 = (s32[128]{0:T(128)S(1)}, s32[128]{0:T(128)}, u32[]{:S(2)}) copy-start(s32[128]{0:T(128)} %get-tuple-element.134) | copy-start | bytes 1540
  259.2 33.2 %copy-start.117 = (s32[128]{0:T(128)S(1)}, s32[128]{0:T(128)}, u32[]{:S(2)}) copy-start(s32[128]{0:T(128)} %get-tuple-element.156) | copy-start | bytes 1540
  259.2 33.7 %copy-start.114 = (s32[128]{0:T(128)S(1)}, s32[128]{0:T(128)}, u32[]{:S(2)}) copy-start(s32[128]{0:T(128)} %get-tuple-element.144) | copy-start | bytes 1540
  259.2 33.7 %copy-start.113 = (s32[128]{0:T(128)S(1)}, s32[128]{0:T(128)}, u32[]{:S(2)}) copy-start(s32[128]{0:T(128)} %get-tuple-element.142) | copy-start | bytes 1540
  259.2 34.9 %copy-start.92 = (f32[2,516]{1,0:T(2,128)S(1)}, f32[2,516]{1,0:T(2,128)}, u32[]{:S(2)}) copy-start(f32[2,516]{1,0:T(2,128)} %param.25) | copy-start | bytes 12388
  259.2 35.0 %copy-start.100 = (f32[172]{0:T(256)S(1)}, f32[172]{0:T(256)}, u32[]{:S(2)}) copy-start(f32[172]{0:T(256)} %param.28) | copy-start | bytes 2068
  259.2 311.0 %all-reduce.39.cloned.1.call-start = ((), (), s32[]{:S(2)}) async-start(), calls=%async_computation.2 | async-start | bytes 4227072 | tf_op jit(solution)/shard_map/psum | solution.py:78
  259.3 35.5 %copy-start.101 = (s32[1024]{0:T(1024)}, s32[1024]{0:T(1024)S(1)}, u32[]{:S(2)}) copy-start(s32[1024]{0:T(1024)S(1)} %pad_clamp_fusion.6) | copy-start | bytes 12292
  261.3 36.7 %copy-start.4 = (u32[2048,172]{1,0:T(8,128)}, u32[2048,172]{1,0:T(8,128)S(1)}, u32[]{:S(2)}) copy-start(u32[2048,172]{1,0:T(8,128)S(1)} %scatter_custom_fusion) | copy-start | bytes 4227076
  261.4 33.4 %copy-start.84 = (s32[3840]{0:T(1024)}, s32[3840]{0:T(1024)S(1)}, u32[]{:S(2)}) copy-start(s32[3840]{0:T(1024)S(1)} %reshape.961) | copy-start | bytes 46084
  263.2 31.6 %copy-start.105 = (s32[384]{0:T(512)}, s32[384]{0:T(512)S(1)}, u32[]{:S(2)}) copy-start(s32[384]{0:T(512)S(1)} %fusion.70) | copy-start | bytes 4612
  300.4 68.0 %copy-start.51 = (f32[128,172]{1,0:T(8,128)}, f32[128,172]{1,0:T(8,128)S(1)}, u32[]{:S(2)}) copy-start(f32[128,172]{1,0:T(8,128)S(1)} %gather_fusion.5) | copy-start | bytes 264196
  303.5 68.6 %copy-start.33 = (f32[128,172]{0,1:T(8,128)}, f32[128,172]{0,1:T(8,128)S(1)}, u32[]{:S(2)}) copy-start(f32[128,172]{0,1:T(8,128)S(1)} %copy.88) | copy-start | bytes 264196
  303.6 68.5 %copy-start.35 = (f32[128,172]{0,1:T(8,128)}, f32[128,172]{0,1:T(8,128)S(1)}, u32[]{:S(2)}) copy-start(f32[128,172]{0,1:T(8,128)S(1)} %copy.89) | copy-start | bytes 264196
  303.6 64.8 %copy-start.75 = (f32[128,100]{1,0:T(8,128)S(1)}, f32[128,100]{1,0:T(8,128)}, u32[]{:S(2)}) copy-start(f32[128,100]{1,0:T(8,128)} %get-tuple-element.150) | copy-start | bytes 153604
  519.0 180.2 %all-reduce.35.cloned.1.call-start = ((), (), s32[]{:S(2)}) async-start(), calls=%async_computation | async-start | bytes 4227072 | tf_op jit(solution)/shard_map/psum | solution.py:78
  570.2 72.7 %copy-start.96 = (f32[172]{0:T(256)S(1)}, f32[172]{0:T(256)}, u32[]{:S(2)}) copy-start(f32[172]{0:T(256)} %multiply_subtract_fusion.13) | copy-start | bytes 2068
  570.2 73.3 %copy-start.91 = (f32[2,516]{1,0:T(2,128)S(1)}, f32[2,516]{1,0:T(2,128)}, u32[]{:S(2)}) copy-start(f32[2,516]{1,0:T(2,128)} %copy-done.90) | copy-start | bytes 12388
  570.2 131.1 %copy-start.22 = (f32[172,172]{1,0:T(8,128)S(1)}, f32[172,172]{1,0:T(8,128)}, u32[]{:S(2)}) copy-start(f32[172,172]{1,0:T(8,128)} %param.26) | copy-start | bytes 355012
  571.9 131.3 %copy-start.23 = (f32[444,516]{0,1:T(8,128)S(1)}, f32[444,516]{0,1:T(8,128)}, u32[]{:S(2)}) copy-start(f32[444,516]{0,1:T(8,128)} %get-tuple-element.72) | copy-start | bytes 2749252
  571.9 72.2 %collective-permute-start.1 = (f32[2048,172]{0,1:T(8,128)}, f32[2048,172]{0,1:T(8,128)}, u32[]{:S(2)}, u32[]{:S(2)}) collective-permute-start(f32[2048,172]{0,1:T(8,128)} %copy.91), channel_id=1, source_target_pairs={{0,4},{4,8},{8,12},{12,16},{16,20},{20,24},{24,28},{28,0},{1,5},{5... | collective-permute-start | bytes 4227080 | tf_op jit(solution)/shard_map/ppermute | solution.py:14
  (95 other events, 394.9 us)
Sparse Core Ops, SparseCore 0:
  204.4 54.5 all-reduce.40
  263.1 103.2 all-reduce.36
  519.1 51.0 all-reduce.38
  574.0 125.0 all-reduce.34
